TPU v7x, 32 devices: a whole 2x2x4 slice. The times are simulated.
32 devices in a mesh: dp: 16 (over z, y, x), seq: 2 (over core).
Axes of the slice: x: 2, y: 2, z: 4, core: 2. Of those that a mesh axis runs over, the one named last changes fastest.
Arguments:
- patches: bfloat16 [32, 256, 768], P('dp', 'seq'), may hold values from -6 to 6
- block_masks: int32 [32, 196], P('dp'), may hold values from 0 to 1, as said below
- split_rows: int32 [32], P('dp'), may hold values from 6 to 8, as said below
- span_order: int32 [2720], replicated, may hold values from 0 to 2719, as said below
- weights: float32 [10880, 768], P('dp')
- teacher: bfloat16 [10880, 768], P('dp')
- first_moment: float32 [10880, 768], P('dp')
- second_moment: float32 [10880, 768], P('dp')
- step_count: int32 [1], replicated, may hold values from 2 to 20
Outputs:
- total_loss: float32 [], replicated
- grad_norm: float32 [], replicated
- updated_weights: float32 [10880, 768], P('dp')
- weights_copy: bfloat16 [10880, 768], P('dp')
- updated_first: float32 [10880, 768], P('dp')
- updated_second: float32 [10880, 768], P('dp')
Inputs may be any that keep to these rules, and one draw needn't show every extreme that they name: `block_masks`: cells are row-major over the 14 x 14 grid; masks come in aligned 2 x 2 blocks of cells. Rows 0 to split_rows - 1 of an image lie on seq index 0 after its CLS slot, the rest on seq index 1 from slot 0. `span_order`: each of 0 to 2719 once.
All inputs are finite; a program needn't handle non-finite values.
Results may differ from a plain program's by a relative error of at most 0.001.
The roundings to bfloat16 on the way count: a program that leaves them out, or rounds other values in their place, can miss the bound.
Values may be sent and summed in bfloat16 or wider, within the bound.
A program may use at most 256 MiB of HBM per device.

v0:
```python
import math
import jax
import jax.numpy as jnp
from jax import lax
from jax.sharding import PartitionSpec as P

D = 768
HEADS = 12
HD = 64
FF = 3072
PP = 768
GRID = 14
SL = 128
CR = 4
BETA = 2.0
CLIP = 0.01
LEARN = 0.03
DECAY = 0.05
BETA_ONE = 0.9
BETA_TWO = 0.999
ADAM_EPS = 1e-08
NORM_EPS = 1e-06


def from_partner(shard, axis, bit):
    return lax.ppermute(shard, axis, [(i, i ^ 1 << bit) for i in range(lax.axis_size(axis))])


def layout():
    return [
        ("cls", 1, (D,)),
        ("mask_tok", 1, (D,)),
        ("b_pe", 1, (D,)),
        ("ln1_g", 1, (D,)),
        ("ln1_b", 1, (D,)),
        ("b_out", 1, (D,)),
        ("ln2_g", 1, (D,)),
        ("ln2_b", 1, (D,)),
        ("b_two", 1, (D,)),
        ("lnf_g", 1, (D,)),
        ("lnf_b", 1, (D,)),
        ("b_head", 1, (D,)),
        ("b_one", FF // D, (FF,)),
        ("w_pe", PP, (PP, D)),
        ("w_qkv", 3 * D, (D, 3 * D)),
        ("w_out", D, (D, D)),
        ("w_one", FF, (D, FF)),
        ("w_two", FF, (FF, D)),
        ("w_head", D, (D, D)),
    ]


def unpack(flat):
    tables = {}
    offset = 0
    for entry_name, entry_rows, entry_shape in layout():
        tables[entry_name] = flat[offset : offset + entry_rows].reshape(entry_shape)
        offset = offset + entry_rows
    return tables


def pack_flat(tables, total_rows):
    pieces = [tables[entry_name].reshape(-1, D) for entry_name, entry_rows, entry_shape in layout()]
    stacked = jnp.concatenate(pieces, 0)
    return jnp.concatenate(
        [stacked, jnp.zeros((total_rows - stacked.shape[0], D), stacked.dtype)], 0
    )


def reorder(stored, order):
    return stored.reshape(order.shape[0], -1, D)[order].reshape(-1, D)


def slot_info(split_rows, seq_side):
    column = jnp.arange(SL)[None, :]
    split_col = split_rows[:, None]
    first_side = seq_side == 0
    first_slot = jnp.where(first_side, 1, 0)
    filled = jnp.where(first_side, split_col * GRID, (GRID - split_col) * GRID)
    offset = jnp.where(first_side, -1, split_col * GRID)
    is_patch = (column >= first_slot) & (column < first_slot + filled)
    is_cls = first_side & (column == 0) & (split_col >= 0)
    grid_cell = jnp.clip(column + offset, 0, GRID * GRID - 1)
    return (is_patch, is_cls, grid_cell)


def sincos(grid_cell):
    quarter = D // 4
    frequency = 1.0 / 10000.0 ** (jnp.arange(quarter).astype(jnp.float32) / quarter)
    rows_at = (grid_cell // GRID).astype(jnp.float32)[..., None] * frequency
    cols_at = (grid_cell % GRID).astype(jnp.float32)[..., None] * frequency
    return jnp.concatenate(
        [jnp.sin(rows_at), jnp.cos(rows_at), jnp.sin(cols_at), jnp.cos(cols_at)], -1
    )


def layer_norm(values):
    center = jnp.mean(values, -1, keepdims=True)
    centred = values - center
    return centred * lax.rsqrt(jnp.mean(centred * centred, -1, keepdims=True) + NORM_EPS)


def matmul_f32(left_mat, right_mat):
    return jnp.dot(left_mat, right_mat, preferred_element_type=jnp.float32)


def weight_grad(left_mat, right_mat):
    return lax.dot_general(
        left_mat, right_mat, (((0,), (0,)), ((), ())), preferred_element_type=jnp.float32
    )


def back_dot(left_mat, right_mat):
    return lax.dot_general(
        left_mat, right_mat, (((1,), (1,)), ((), ())), preferred_element_type=jnp.float32
    )


def vector(params, entry_name):
    return params[entry_name].astype(jnp.float32)


def column_sums(values):
    return jnp.sum(values.astype(jnp.float32), 0)


def norm_fwd(values, gain_vec, bias_vec):
    center = jnp.mean(values, -1, keepdims=True)
    centred = values - center
    inverse = lax.rsqrt(jnp.mean(centred * centred, -1, keepdims=True) + NORM_EPS)
    normed = centred * inverse
    return (normed * gain_vec + bias_vec, normed, inverse)


def norm_back(grad_out, normed, inverse, gain_vec):
    scaled = grad_out * gain_vec
    grad_in = inverse * (
        scaled
        - jnp.mean(scaled, -1, keepdims=True)
        - normed * jnp.mean(scaled * normed, -1, keepdims=True)
    )
    return (grad_in, jnp.sum(grad_out * normed, 0), jnp.sum(grad_out, 0))


def place_tokens(params, embedded, is_patch, is_cls, hidden_mask, position):
    on_grid = embedded.reshape(is_patch.shape + (D,)) + position
    tokens = jnp.where(is_patch[..., None], on_grid, 0.0)
    tokens = jnp.where(hidden_mask[..., None], vector(params, "mask_tok") + position, tokens)
    tokens = jnp.where(is_cls[..., None], vector(params, "cls"), tokens)
    return tokens.reshape(-1, D)


def project(params, tokens, length):
    normed_in, normed, inverse = norm_fwd(tokens, vector(params, "ln1_g"), vector(params, "ln1_b"))
    normed_in = normed_in.astype(jnp.bfloat16)
    packed = (
        matmul_f32(normed_in, params["w_qkv"])
        .astype(jnp.bfloat16)
        .reshape(-1, length, 3, HEADS, HD)
    )
    return (normed_in, normed, inverse, packed[:, :, 0], packed[:, :, 1], packed[:, :, 2])


def scores_of(queries, keys_block, key_live):
    raw_scores = jnp.einsum(
        "bqhd,bkhd->bhqk", queries, keys_block, preferred_element_type=jnp.float32
    ) * HD ** (-0.5)
    return jnp.where(key_live[:, None, None, :], raw_scores, -1e30)


def attend(queries, blocks):
    scores = [scores_of(queries, block[0], block[2]) for block in blocks]
    highest = reduce_max([jnp.max(member, -1, keepdims=True) for member in scores])
    summed = sum([jnp.sum(jnp.exp(member - highest), -1, keepdims=True) for member in scores])
    logsum = highest + jnp.log(summed)
    mixed_out = sum(
        [
            jnp.einsum(
                "bhqk,bkhd->bqhd",
                jnp.exp(member - logsum).astype(jnp.bfloat16),
                block[1],
                preferred_element_type=jnp.float32,
            )
            for member, block in zip(scores, blocks)
        ]
    )
    return (mixed_out.astype(jnp.bfloat16).reshape(-1, D), logsum)


def reduce_max(members):
    highest = members[0]
    for member in members[1:]:
        highest = jnp.maximum(highest, member)
    return highest


def finish(params, tokens, queries, blocks):
    mixed_out, logsum = attend(queries, blocks)
    hidden = tokens + matmul_f32(mixed_out, params["w_out"]) + vector(params, "b_out")
    normed_two_in, normed_two, inverse_two = norm_fwd(
        hidden, vector(params, "ln2_g"), vector(params, "ln2_b")
    )
    normed_two_in = normed_two_in.astype(jnp.bfloat16)
    upward = matmul_f32(normed_two_in, params["w_one"]) + vector(params, "b_one")
    gelled = jax.nn.gelu(upward).astype(jnp.bfloat16)
    output = hidden + matmul_f32(gelled, params["w_two"]) + vector(params, "b_two")
    return (output, (mixed_out, logsum, normed_two, inverse_two, normed_two_in, upward, gelled))


def layer_back(params, grad_out, saved, far_blocks, key_live, gradients):
    (
        normed_in,
        normed,
        inverse,
        queries,
        keys_loc,
        values_loc,
        mixed_out,
        logsum,
        normed_two,
        inverse_two,
        normed_two_in,
        upward,
        gelled,
    ) = saved
    length = queries.shape[1]
    blocks = [(keys_loc, values_loc, key_live)] + far_blocks
    grad_branch = grad_out.astype(jnp.bfloat16)
    gradients["w_two"] = weight_grad(gelled, grad_branch)
    gradients["b_two"] = column_sums(grad_branch)
    unused, gelu_pull = jax.vjp(jax.nn.gelu, upward)
    grad_up = gelu_pull(back_dot(grad_branch, params["w_two"]))[0].astype(jnp.bfloat16)
    gradients["w_one"] = weight_grad(normed_two_in, grad_up)
    gradients["b_one"] = column_sums(grad_up)
    grad_two, gradients["ln2_g"], gradients["ln2_b"] = norm_back(
        back_dot(grad_up, params["w_one"]), normed_two, inverse_two, vector(params, "ln2_g")
    )
    grad_hidden = grad_out + grad_two
    grad_attn = grad_hidden.astype(jnp.bfloat16)
    gradients["w_out"] = weight_grad(mixed_out, grad_attn)
    gradients["b_out"] = column_sums(grad_attn)
    grad_mixed = (
        back_dot(grad_attn, params["w_out"]).astype(jnp.bfloat16).reshape(-1, length, HEADS, HD)
    )
    probs = [jnp.exp(scores_of(queries, block[0], block[2]) - logsum) for block in blocks]
    pushes = [
        jnp.einsum("bqhd,bkhd->bhqk", grad_mixed, block[1], preferred_element_type=jnp.float32)
        for block in blocks
    ]
    common = sum([jnp.sum(prob * push, -1, keepdims=True) for prob, push in zip(probs, pushes)])
    grad_scores = [
        (prob * (push - common)).astype(jnp.bfloat16) for prob, push in zip(probs, pushes)
    ]
    key_scale = HD ** (-0.5)
    grad_queries = (
        sum(
            [
                jnp.einsum("bhqk,bkhd->bqhd", member, block[0], preferred_element_type=jnp.float32)
                for member, block in zip(grad_scores, blocks)
            ]
        )
        * key_scale
    )
    key_grads = [
        jnp.einsum("bhqk,bqhd->bkhd", member, queries, preferred_element_type=jnp.float32)
        * key_scale
        for member in grad_scores
    ]
    value_grads = [
        jnp.einsum(
            "bhqk,bqhd->bkhd",
            prob.astype(jnp.bfloat16),
            grad_mixed,
            preferred_element_type=jnp.float32,
        )
        for prob in probs
    ]
    grad_keys, grad_values = (key_grads[0], value_grads[0])
    returned = from_partner(
        jnp.stack([key_grads[1], value_grads[1]]).astype(jnp.bfloat16), "seq", 0
    ).astype(jnp.float32)
    grad_keys = grad_keys + returned[0]
    grad_values = grad_values + returned[1]
    grad_packed = (
        jnp.stack([grad_queries, grad_keys, grad_values], 2).astype(jnp.bfloat16).reshape(-1, 3 * D)
    )
    gradients["w_qkv"] = weight_grad(normed_in, grad_packed)
    grad_first, gradients["ln1_g"], gradients["ln1_b"] = norm_back(
        back_dot(grad_packed, params["w_qkv"]), normed, inverse, vector(params, "ln1_g")
    )
    return grad_hidden + grad_first


def on_device(
    patches,
    block_masks,
    split_rows,
    span_order,
    weights,
    teacher,
    first_moment,
    second_moment,
    step_count,
):
    gathered, teacher_all = (
        lax.all_gather(weights.astype(jnp.bfloat16), "dp", axis=0, tiled=True),
        lax.all_gather(teacher, "dp", axis=0, tiled=True),
    )
    inverse_order = jnp.argsort(span_order)
    params = unpack(reorder(gathered, inverse_order))
    teacher_params = unpack(reorder(teacher_all, inverse_order))
    seq_side = lax.axis_index("seq")
    is_patch, is_cls, grid_cell = slot_info(split_rows, seq_side)
    far_patch, far_cls, far_cell = slot_info(split_rows, 1 - seq_side)
    far_live = far_patch | far_cls
    length = SL
    images = patches.shape[0]
    hidden_mask = (jnp.take_along_axis(block_masks, grid_cell, 1) == 1) & is_patch
    key_live = is_patch | is_cls
    masked_count = lax.psum(jnp.sum(hidden_mask.astype(jnp.float32)), ("dp", "seq"))
    position = sincos(grid_cell)
    pixels = patches.reshape(-1, PP)
    embedded_teacher = matmul_f32(pixels, teacher_params["w_pe"]) + vector(teacher_params, "b_pe")
    embedded_student = matmul_f32(pixels, params["w_pe"]) + vector(params, "b_pe")
    tokens_teacher = place_tokens(
        teacher_params, embedded_teacher, is_patch, is_cls, jnp.zeros_like(hidden_mask), position
    )
    tokens_student = place_tokens(params, embedded_student, is_patch, is_cls, hidden_mask, position)
    teacher_proj = project(teacher_params, tokens_teacher, length)
    student_proj = project(params, tokens_student, length)
    arrived = from_partner(
        jnp.stack([teacher_proj[4], teacher_proj[5], student_proj[4], student_proj[5]]), "seq", 0
    )
    teacher_far = [(arrived[0], arrived[1], far_live)]
    student_far = [(arrived[2], arrived[3], far_live)]
    teacher_out, unused = finish(
        teacher_params,
        tokens_teacher,
        teacher_proj[3],
        [(teacher_proj[4], teacher_proj[5], key_live)] + teacher_far,
    )
    target = layer_norm(teacher_out)
    student_out, finish_saved = finish(
        params,
        tokens_student,
        student_proj[3],
        [(student_proj[4], student_proj[5], key_live)] + student_far,
    )
    final_in, final_normed, final_inverse = norm_fwd(
        student_out, vector(params, "lnf_g"), vector(params, "lnf_b")
    )
    final_in = final_in.astype(jnp.bfloat16)
    predicted = matmul_f32(final_in, params["w_head"]) + vector(params, "b_head")
    difference = predicted - target
    magnitude = jnp.abs(difference)
    elementwise = jnp.where(
        magnitude < BETA, 0.5 * difference * difference / BETA, magnitude - 0.5 * BETA
    )
    selected = hidden_mask.reshape(-1)[:, None]
    loss_scale = 1.0 / (math.sqrt(D) * masked_count)
    total_loss = lax.psum(
        jnp.sum(jnp.where(selected, elementwise, 0.0)) * loss_scale, ("dp", "seq")
    )
    grad_pred = (
        jnp.where(selected, jnp.clip(difference / BETA, -1.0, 1.0), 0.0) * loss_scale
    ).astype(jnp.bfloat16)
    gradients = {}
    gradients["w_head"] = weight_grad(final_in, grad_pred)
    gradients["b_head"] = column_sums(grad_pred)
    grad_tokens, gradients["lnf_g"], gradients["lnf_b"] = norm_back(
        back_dot(grad_pred, params["w_head"]), final_normed, final_inverse, vector(params, "lnf_g")
    )
    saved = tuple(student_proj) + tuple(finish_saved)
    grad_tokens = layer_back(params, grad_tokens, saved, student_far, key_live, gradients)
    grad_slots = grad_tokens.reshape(images, length, D)
    visible = (is_patch & jnp.logical_not(hidden_mask))[..., None]
    grad_embed = jnp.where(visible, grad_slots, 0.0).astype(jnp.bfloat16).reshape(-1, D)
    gradients["w_pe"] = weight_grad(pixels, grad_embed)
    gradients["b_pe"] = column_sums(grad_embed)
    gradients["mask_tok"] = jnp.sum(jnp.where(hidden_mask[..., None], grad_slots, 0.0), (0, 1))
    gradients["cls"] = jnp.sum(jnp.where(is_cls[..., None], grad_slots, 0.0), (0, 1))
    stored_grad = reorder(pack_flat(gradients, span_order.shape[0] * CR), span_order)
    owned_grad = lax.psum_scatter(stored_grad, "dp", scatter_dimension=0, tiled=True)
    owned_grad = lax.psum(owned_grad, "seq")
    squares = lax.psum(jnp.sum(owned_grad * owned_grad), "dp")
    grad_norm = jnp.sqrt(squares)
    clipped = owned_grad * (CLIP / jnp.maximum(grad_norm, CLIP))
    updated_first = BETA_ONE * first_moment + (1.0 - BETA_ONE) * clipped
    updated_second = BETA_TWO * second_moment + (1.0 - BETA_TWO) * clipped * clipped
    steps_done = step_count[0].astype(jnp.float32)
    adam_step = (
        updated_first
        / (1.0 - BETA_ONE**steps_done)
        / (jnp.sqrt(updated_second / (1.0 - BETA_TWO**steps_done)) + ADAM_EPS)
    )
    updated_weights = weights - LEARN * (adam_step + DECAY * weights)
    return (
        total_loss,
        grad_norm,
        updated_weights,
        updated_weights.astype(jnp.bfloat16),
        updated_first,
        updated_second,
    )


def solution(mesh):
    placed = (
        P("dp", "seq", None),
        P("dp", None),
        P("dp"),
        P(),
        P("dp", None),
        P("dp", None),
        P("dp", None),
        P("dp", None),
        P(),
    )
    return jax.shard_map(
        on_device,
        mesh=mesh,
        in_specs=placed,
        out_specs=(P(), P(), P("dp", None), P("dp", None), P("dp", None), P("dp", None)),
        check_vma=False,
    )
```

profile of v0, /device:TPU:0, one launch (start us, length us, event | category | flops | bytes accessed | tf_op | source)
XLA Modules:
  0.0 1527.9 jit_solution(8221068962807406303)
XLA Ops:
  14.6 44.4 %psum.28 = f32[]{:T(128)} all-reduce(f32[]{:T(128)} %convert_reduce_fusion.5), channel_id=1, replica_groups=mesh['dp'=16,'seq'=2] {'dp','seq'}, use_global_device_ids=true, to_apply=%region_23.24 | all-reduce | flops 1 | bytes 8 | tf_op jit(solution)/shard_map/psum | solution.py:320
  59.7 5.8 sort.17
  70.2 135.1 %all-gather.5.cloned.1.call-done = bf16[10880,768]{1,0:T(8,128)(2,1)} async-done(((bf16[680,768]{1,0:T(8,128)(2,1)}), bf16[10880,768]{1,0:T(8,128)(2,1)}) %all-gather.5.cloned.1.call-update) | async-done | bytes 16711696 | tf_op jit(solution)/shard_map/all_gather | solution.py:307
  205.3 28.0 %reshape.817 = bf16[2720,4,768]{2,1,0:T(4,128)(2,1)} reshape(bf16[10880,768]{1,0:T(8,128)(2,1)} %all-gather.5.cloned.1.call-done) | data formatting | bytes 33423360 | tf_op jit(solution)/shard_map/reshape | solution.py:71
  233.4 26.2 %gather_fusion.1 = bf16[2720,4,768]{2,1,0:T(4,128)(2,1)} fusion(bf16[2720,4,768]{2,1,0:T(4,128)(2,1)} %reshape.817, s32[3072]{0:T(1024)S(1)} %pad_clamp_fusion.1), kind=kCustom, calls=%fused_computation.1 | custom fusion | bytes 33434240 | tf_op jit(solution)/shard_map/gather | solution.py:71
  259.6 26.7 %reshape.818 = bf16[10880,768]{1,0:T(8,128)(2,1)} reshape(bf16[2720,4,768]{2,1,0:T(4,128)(2,1)} %gather_fusion.1) | data formatting | bytes 33423360 | tf_op jit(solution)/shard_map/reshape | solution.py:71
  295.2 102.2 %all-gather.3.cloned.1.call-done = bf16[10880,768]{1,0:T(8,128)(2,1)} async-done(((bf16[680,768]{1,0:T(8,128)(2,1)}), bf16[10880,768]{1,0:T(8,128)(2,1)}) %all-gather.3.cloned.1.call-update) | async-done | bytes 16711696 | tf_op jit(solution)/shard_map/all_gather | solution.py:306
  397.3 27.9 %reshape.812 = bf16[2720,4,768]{2,1,0:T(4,128)(2,1)} reshape(bf16[10880,768]{1,0:T(8,128)(2,1)} %all-gather.3.cloned.1.call-done) | data formatting | bytes 33423360 | tf_op jit(solution)/shard_map/reshape | solution.py:71
  425.2 26.4 %gather_fusion = bf16[2720,4,768]{2,1,0:T(4,128)(2,1)} fusion(bf16[2720,4,768]{2,1,0:T(4,128)(2,1)} %reshape.812, s32[3072]{0:T(1024)S(1)} %pad_clamp_fusion.1), kind=kCustom, calls=%fused_computation | custom fusion | bytes 33434240 | tf_op jit(solution)/shard_map/gather | solution.py:71
  456.7 26.6 %reshape.813 = bf16[10880,768]{1,0:T(8,128)(2,1)} reshape(bf16[2720,4,768]{2,1,0:T(4,128)(2,1)} %gather_fusion) | data formatting | bytes 33423360 | tf_op jit(solution)/shard_map/reshape | solution.py:71
  487.6 10.6 fusion.163
  507.4 17.8 %reshape.819 = bf16[768,2304]{1,0:T(8,128)(2,1)} reshape(bf16[576,4,768]{2,1,0:T(4,128)(2,1)} %slice.238) | data formatting | bytes 7077888 | tf_op jit(solution)/shard_map/reshape | solution.py:57
  539.6 7.2 reshape.815
  567.6 8.5 slice.211
  576.1 5.5 copy.83
  584.5 10.5 fusion.161
  595.1 9.0 slice.193
  604.1 5.6 copy.81
  619.0 7.5 fusion.172
  661.6 5.2 fusion.156
  679.1 11.8 reshape.841
  692.3 7.7 fusion.145
  711.9 8.4 reshape.840
  722.5 78.6 %concatenate.9 = f32[10880,768]{1,0:T(8,128)} concatenate(f32[1,768]{1,0:T(1,128)S(1)} %reshape.826, f32[1,768]{1,0:T(1,128)S(1)} %reshape.827, f32[1,768]{1,0:T(1,128)S(1)} %reshape.828, f32[1,768]{1,0:T(1,128)S(1)} %reshape.829, f32[1,768]{1,0:T(1,128)S(1)} %reshape.830, f32[1,768]{1,0:T(1,128)S(1)} %copy-done.82, f32[1,768]{1,0:T(1,128)S(1)} %copy-done.83, ...), dimensions={0} | concatenate | bytes 66846720 | tf_op jit(solution)/shard_map/concatenate | solution.py:65
  801.1 37.8 %reshape.842 = f32[2720,4,768]{2,1,0:T(4,128)} reshape(f32[10880,768]{1,0:T(8,128)} %concatenate.9) | data formatting | bytes 66846720 | tf_op jit(solution)/shard_map/reshape | solution.py:71
  838.9 32.6 %gather_fusion.2 = f32[2720,4,768]{2,1,0:T(4,128)} fusion(f32[2720,4,768]{2,1,0:T(4,128)} %reshape.842, s32[3072]{0:T(1024)S(1)} %copy-done.60), kind=kCustom, calls=%fused_computation.2 | custom fusion | bytes 66857600 | tf_op jit(solution)/shard_map/gather | solution.py:71
  871.5 38.5 %reshape.843 = f32[10880,768]{1,0:T(8,128)} reshape(f32[2720,4,768]{2,1,0:T(4,128)} %gather_fusion.2) | data formatting | bytes 66846720 | tf_op jit(solution)/shard_map/reshape | solution.py:71
  910.1 494.6 %reduce-scatter.2.cloned.1.call-done = f32[680,768]{1,0:T(8,128)} async-done(((f32[10880,768]{1,0:T(8,128)}), f32[680,768]{1,0:T(8,128)}) %reduce-scatter.2.cloned.1.call-update) | async-done | bytes 2088976 | tf_op jit(solution)/shard_map/reduce_scatter | solution.py:383
  1406.3 21.3 %all-reduce.2.cloned.1.call-done = f32[680,768]{1,0:T(8,128)} async-done(((f32[680,768]{1,0:T(8,128)}), f32[680,768]{1,0:T(8,128)}) %all-reduce.2.cloned.1.call-update) | async-done | bytes 2088976 | tf_op jit(solution)/shard_map/psum | solution.py:384
  1430.3 40.5 %psum.29 = f32[]{:T(128)} all-reduce(f32[]{:T(128)S(6)} %mul.479), channel_id=1, replica_groups=mesh['dp'=16,'seq'=2] {'dp','seq'}, use_global_device_ids=true, to_apply=%region_24.25 | all-reduce | flops 1 | bytes 8 | tf_op jit(solution)/shard_map/psum | solution.py:361
  1470.8 41.3 %psum.31 = f32[]{:T(128)} all-reduce(f32[]{:T(128)} %multiply_reduce_fusion), channel_id=1, replica_groups=mesh['dp'=16,'seq'=2] {'dp'}, use_global_device_ids=true, to_apply=%region_49.50 | all-reduce | flops 1 | bytes 8 | tf_op jit(solution)/shard_map/psum | solution.py:385
  1512.9 6.9 fusion.158
  (379 shorter events, 150.9 us)
Async XLA Ops:
  7.2 518.1 %copy-start = (bf16[2,128,768]{2,1,0:T(8,128)(2,1)S(1)}, bf16[2,128,768]{2,1,0:T(8,128)(2,1)}, u32[]{:S(2)}) copy-start(bf16[2,128,768]{2,1,0:T(8,128)(2,1)} %param.9) | copy-start | bytes 1179652
  7.2 198.1 %all-gather.5.cloned.1.call-start = ((), (), s32[]{:S(2)}) async-start(), calls=%async_computation.2 | async-start | bytes 17756160 | tf_op jit(solution)/shard_map/all_gather | solution.py:307
  7.9 51.8 %copy-start.61 = (s32[2720]{0:T(1024)S(1)}, s32[2720]{0:T(1024)}, u32[]{:S(2)}) copy-start(s32[2720]{0:T(1024)} %param.12) | copy-start | bytes 32644
  7.9 389.4 %all-gather.3.cloned.1.call-start = ((), (), s32[]{:S(2)}) async-start(), calls=%async_computation.1 | async-start | bytes 17756160 | tf_op jit(solution)/shard_map/all_gather | solution.py:306
  10.7 1394.1 %reduce-scatter.2.cloned.1.call-start = ((), (), s32[]{:S(2)}) async-start(), calls=%async_computation.3 | async-start | bytes 35512320 | tf_op jit(solution)/shard_map/reduce_scatter | solution.py:383
  548.6 5.6 copy-start.54
  548.6 5.6 copy-start.58
  565.1 46.4 %copy-start.31 = (bf16[2,128,1,12,64]{1,0,4,3,2:T(2,128)(2,1)}, bf16[2,128,1,12,64]{1,0,4,3,2:T(2,128)(2,1)S(1)}, u32[]{:S(2)}) copy-start(bf16[2,128,1,12,64]{1,0,4,3,2:T(2,128)(2,1)S(1)} %get-tuple-element.74) | copy-start | bytes 1179652
  565.1 46.4 %copy-start.34 = (bf16[2,128,1,12,64]{1,0,4,3,2:T(2,128)(2,1)}, bf16[2,128,1,12,64]{1,0,4,3,2:T(2,128)(2,1)S(1)}, u32[]{:S(2)}) copy-start(bf16[2,128,1,12,64]{1,0,4,3,2:T(2,128)(2,1)S(1)} %get-tuple-element.76) | copy-start | bytes 1179652
  567.6 45.1 %collective-permute-start = (bf16[4,2,128,12,64]{2,4,3,1,0:T(8,128)(2,1)}, bf16[4,2,128,12,64]{2,4,3,1,0:T(8,128)(2,1)}, u32[]{:S(2)}, u32[]{:S(2)}) collective-permute-start(bf16[4,2,128,12,64]{2,4,3,1,0:T(8,128)(2,1)} %pad_maximum_fusion), channel_id=1, source_target_pairs={{0,1},{1,0},{2,3},{3,2},{4,5},{5,4},{6,7},{7,6},{8,9},{9,8},{10,11... | collective-permute-start | bytes 4718600 | tf_op jit(solution)/shard_map/ppermute | solution.py:26
  576.1 5.5 copy-start.62
  604.0 6.9 copy-start.43
  604.0 6.9 copy-start.49
  604.1 6.9 copy-start.106
  632.5 5.7 slice-start.2
  633.1 17.3 %copy-start.8 = (f32[256,768]{1,0:T(8,128)}, f32[256,768]{1,0:T(8,128)S(1)}, u32[]{:S(2)}) copy-start(f32[256,768]{1,0:T(8,128)S(1)} %get-tuple-element.114) | copy-start | bytes 2359300
  633.2 17.2 %copy-start.68 = (f32[256]{0:T(256)}, f32[256]{0:T(256)S(1)}, u32[]{:S(2)}) copy-start(f32[256]{0:T(256)S(1)} %broadcast_multiply_fusion.9) | copy-start | bytes 3076
  633.4 17.0 %copy-start.80 = (f32[256]{0:T(256)}, f32[256]{0:T(256)S(1)}, u32[]{:S(2)}) copy-start(f32[256]{0:T(256)S(1)} %add_rsqrt_fusion.3) | copy-start | bytes 3076
  638.2 6.2 copy-start.26
  644.4 6.0 copy-start.15
  661.6 5.3 copy-start.18
  661.6 5.3 copy-start.51
  661.6 5.3 copy-start.65
  661.6 5.2 copy-start.73
  672.5 5.4 copy-start.95
  672.5 6.0 copy-start.90
  673.4 26.6 %collective-permute-start.1 = (bf16[2,2,128,12,64]{2,4,3,1,0:T(8,128)(2,1)}, bf16[2,2,128,12,64]{2,4,3,1,0:T(8,128)(2,1)}, u32[]{:S(2)}, u32[]{:S(2)}) collective-permute-start(bf16[2,2,128,12,64]{2,4,3,1,0:T(8,128)(2,1)} %pad_maximum_fusion.2), channel_id=1, source_target_pairs={{0,1},{1,0},{2,3},{3,2},{4,5},{5,4},{6,7},{7,6},{8,9},{9,8},{10,11... | collective-permute-start | bytes 2359304 | tf_op jit(solution)/shard_map/ppermute | solution.py:26
  679.1 11.8 copy-start.20
  711.8 8.5 copy-start.102
  801.1 37.8 %copy-start.60 = (s32[3072]{0:T(1024)S(1)}, s32[3072]{0:T(1024)}, u32[]{:S(2)}) copy-start(s32[3072]{0:T(1024)} %pad_clamp_fusion) | copy-start | bytes 36868
  910.0 517.6 %all-reduce.2.cloned.1.call-start = ((), (), s32[]{:S(2)}) async-start(), calls=%async_computation.4 | async-start | bytes 4177920 | tf_op jit(solution)/shard_map/psum | solution.py:384
  1404.7 108.1 %copy-start.14 = (f32[680,768]{1,0:T(8,128)S(1)}, f32[680,768]{1,0:T(8,128)}, u32[]{:S(2)}) copy-start(f32[680,768]{1,0:T(8,128)} %param.13) | copy-start | bytes 6266884
  (88 other events, 211.6 us)
Sparse Core Ops, SparseCore 0:
  10.8 194.4 all-gather.4
  208.7 188.5 all-gather.2
  910.2 494.5 reduce-scatter.1
  1406.9 20.6 all-reduce.1
where the time goes:
time: 1550 us; the launch traced here: 1530 us
  waiting for transfers between devices  754 us (49%)
  local copies, waits for them, and re-layouts  512 us (33%)
  blocking collectives  126 us (8%)
  matrix products  74.8 us (5%)
  other arithmetic  40.3 us (3%)
  between operations  19.9 us (1%)
    reduce_scatter x1, waiting for transfers between devices, on_device(): lax.psum_scatter(stored_grad, 'dp', scatter_dimension=0, tiled=True)  495 us
    reshape x6, local copies, waits for them, and re-layouts, reorder(): return stored.reshape(order.shape[0], -1, D)[order].reshape(-1, D)  186 us
    all_gather x1, waiting for transfers between devices, on_device(): lax.all_gather(teacher, 'dp', axis=0, tiled=True)  135 us
    all_gather x1, waiting for transfers between devices, on_device(): lax.all_gather(weights.astype(jnp.bfloat16), 'dp', axis=0, tiled=True)  102 us
    gather x3, local copies, waits for them, and re-layouts, reorder(): return stored.reshape(order.shape[0], -1, D)[order].reshape(-1, D)  85.2 us
    concatenate x1, local copies, waits for them, and re-layouts, pack_flat(): jnp.concatenate([stacked, jnp.zeros((total_rows - stacked.shape[0], D), s...  78.6 us
    slice x13, local copies, waits for them, and re-layouts, unpack(): tables[entry_name] = flat[offset:offset + entry_rows].reshape(entry_shape)  68.6 us
    psum x1, blocking collectives, on_device(): lax.psum(jnp.sum(hidden_mask.astype(jnp.float32)), ('dp', 'seq'))  44.4 us
  transfers between devices with their start and end apart: 6, of which 4 were waited for; matrix products, arithmetic and copies ran while one was open for 12% of the time, Pallas kernels for 0%

commit v1 on v0

--- a/solution.py
+++ b/solution.py
@@ -20,6 +20,28 @@
 BETA_TWO = 0.999
 ADAM_EPS = 1e-08
 NORM_EPS = 1e-06
+
+
+def joined_along(blocks, dim):
+    shape = list(blocks.shape[1:])
+    shape[dim] *= blocks.shape[0]
+    return jnp.moveaxis(blocks, 0, dim).reshape(shape)
+
+
+def gather_around(value, axis, dim):
+    size = lax.axis_size(axis)
+    pairs = [(i, (i + 1) % size) for i in range(size)]
+    back = [(b, a) for a, b in pairs]
+    lower, upper = ([], [])
+    for turn in range(size - 1):
+        if turn % 2 == 0:
+            lower.append(lax.ppermute(lower[-1] if lower else value, axis, pairs))
+        else:
+            upper.append(lax.ppermute(upper[-1] if upper else value, axis, back))
+    tiles = jnp.stack([*lower[::-1], value, *upper])
+    shift = lax.axis_index(axis) - len(lower)
+    tiles = tiles[(jnp.arange(size) - shift) % size]
+    return joined_along(tiles, dim)
 
 
 def from_partner(shard, axis, bit):
@@ -304,7 +326,7 @@
 ):
     gathered, teacher_all = (
         lax.all_gather(weights.astype(jnp.bfloat16), "dp", axis=0, tiled=True),
-        lax.all_gather(teacher, "dp", axis=0, tiled=True),
+        gather_around(teacher, "dp", 0),
     )
     inverse_order = jnp.argsort(span_order)
     params = unpack(reorder(gathered, inverse_order))

time: 1550 us -> 1750 us (1.13)
  waiting for transfers between devices: 754 us -> 825 us
  starting transfers between devices: 0.66 us -> 63.7 us
  blocking collectives: 126 us -> 169 us
  local copies, waits for them, and re-layouts: 512 us -> 537 us
    ppermute x0 -> x15, waiting for transfers between devices: none -> 309 us  [the longest x8 261 us: gather_around(): lower.append(lax.ppermute(lower[-1] if lower else value, axis, pairs))]
    all_gather x1 -> x0, waiting for transfers between devices: 135 us -> none  [on_device(): lax.all_gather(teacher, 'dp', axis=0, tiled=True)]
    all_gather x1, waiting for transfers between devices: 102 us -> 0.01 us  [on_device(): lax.all_gather(weights.astype(jnp.bfloat16), 'dp', axis=0, tiled=True)]
    ppermute x0 -> x15, starting transfers between devices: none -> 63.1 us  [the longest x8 46.7 us: gather_around(): lower.append(lax.ppermute(lower[-1] if lower else value, axis, pairs))]
    psum x1, blocking collectives: 44.4 us -> 86.9 us  [on_device(): lax.psum(jnp.sum(hidden_mask.astype(jnp.float32)), ('dp', 'seq'))]
    another operation x0 -> x2, local copies, waits for them, and re-layouts: none -> 29 us  [the longest x1 27.9 us: reorder(): return stored.reshape(order.shape[0], -1, D)[order].reshape(-1, D)]
    unnamed x234 -> x283, local copies, waits for them, and re-layouts: 17.1 us -> 46 us
    reshape x6 -> x5, local copies, waits for them, and re-layouts: 186 us -> 158 us  [reorder(): return stored.reshape(order.shape[0], -1, D)[order].reshape(-1, D)]
  transfers between devices with their start and end apart: 6 -> 20, of which waited for: 4 -> 11; matrix products, arithmetic and copies ran while one was open for 12% -> 15% of each run, Pallas kernels for 0% -> 0%
where the time goes in v1:
time: 1750 us; the launch traced here: 1740 us
  waiting for transfers between devices  825 us (47%)
  local copies, waits for them, and re-layouts  537 us (31%)
  blocking collectives  169 us (10%)
  matrix products  74.3 us (4%)
  starting transfers between devices  63.7 us (4%)
  other arithmetic  49.5 us (3%)
  between operations  19.8 us (1%)
    reduce_scatter x1, waiting for transfers between devices, on_device(): lax.psum_scatter(stored_grad, 'dp', scatter_dimension=0, tiled=True)  494 us
    ppermute x8, waiting for transfers between devices, gather_around(): lower.append(lax.ppermute(lower[-1] if lower else value, axis, pairs))  261 us
    reshape x5, local copies, waits for them, and re-layouts, reorder(): return stored.reshape(order.shape[0], -1, D)[order].reshape(-1, D)  158 us
    psum x1, blocking collectives, on_device(): lax.psum(jnp.sum(hidden_mask.astype(jnp.float32)), ('dp', 'seq'))  86.9 us
    gather x3, local copies, waits for them, and re-layouts, reorder(): return stored.reshape(order.shape[0], -1, D)[order].reshape(-1, D)  84.9 us
    concatenate x1, local copies, waits for them, and re-layouts, pack_flat(): jnp.concatenate([stacked, jnp.zeros((total_rows - stacked.shape[0], D), s...  78.6 us
    slice x13, local copies, waits for them, and re-layouts, unpack(): tables[entry_name] = flat[offset:offset + entry_rows].reshape(entry_shape)  67.5 us
    ppermute x7, waiting for transfers between devices, gather_around(): upper.append(lax.ppermute(upper[-1] if upper else value, axis, back))  48.8 us
  transfers between devices with their start and end apart: 20, of which 11 were waited for; matrix products, arithmetic and copies ran while one was open for 15% of the time, Pallas kernels for 0%

profile of v1, /device:TPU:0, one launch (start us, length us, event | category | flops | bytes accessed | tf_op | source)
XLA Modules:
  0.0 1737.9 jit_solution(12124418705771011849)
XLA Ops:
  13.1 38.7 %collective-permute-done = bf16[680,768]{1,0:T(8,128)(2,1)S(1)} collective-permute-done((bf16[680,768]{1,0:T(8,128)(2,1)S(1)}, bf16[680,768]{1,0:T(8,128)(2,1)S(1)}, u32[]{:S(2)}, u32[]{:S(2)}) %collective-permute-start) | collective-permute-done | bytes 1044512 | tf_op jit(solution)/shard_map/ppermute | solution.py:38
  57.4 81.8 %collective-permute-done.1 = bf16[680,768]{1,0:T(8,128)(2,1)S(1)} collective-permute-done((bf16[680,768]{1,0:T(8,128)(2,1)S(1)}, bf16[680,768]{1,0:T(8,128)(2,1)S(1)}, u32[]{:S(2)}, u32[]{:S(2)}) %collective-permute-start.1) | collective-permute-done | bytes 1044512 | tf_op jit(solution)/shard_map/ppermute | solution.py:38
  144.9 25.2 %collective-permute-done.2 = bf16[680,768]{1,0:T(8,128)(2,1)S(1)} collective-permute-done((bf16[680,768]{1,0:T(8,128)(2,1)S(1)}, bf16[680,768]{1,0:T(8,128)(2,1)S(1)}, u32[]{:S(2)}, u32[]{:S(2)}) %collective-permute-start.2) | collective-permute-done | bytes 1044512 | tf_op jit(solution)/shard_map/ppermute | solution.py:38
  170.1 24.5 %collective-permute-start.3 = (bf16[680,768]{1,0:T(8,128)(2,1)S(1)}, bf16[680,768]{1,0:T(8,128)(2,1)S(1)}, u32[]{:S(2)}, u32[]{:S(2)}) collective-permute-start(bf16[680,768]{1,0:T(8,128)(2,1)S(1)} %collective-permute-done.2), channel_id=1, source_target_pairs={{0,2},{2,4},{4,6},{6,8},{8,10},{10,12},{12,14},{14,16},{16,18},{18... | collective-permute-start | bytes 3133448 | tf_op jit(solution)/shard_map/ppermute | solution.py:38
  195.5 43.9 %collective-permute-done.3 = bf16[680,768]{1,0:T(8,128)(2,1)S(1)} collective-permute-done((bf16[680,768]{1,0:T(8,128)(2,1)S(1)}, bf16[680,768]{1,0:T(8,128)(2,1)S(1)}, u32[]{:S(2)}, u32[]{:S(2)}) %collective-permute-start.3) | collective-permute-done | bytes 1044512 | tf_op jit(solution)/shard_map/ppermute | solution.py:38
  241.9 30.6 %collective-permute-done.10 = bf16[680,768]{1,0:T(8,128)(2,1)} collective-permute-done((bf16[680,768]{1,0:T(8,128)(2,1)S(1)}, bf16[680,768]{1,0:T(8,128)(2,1)}, u32[]{:S(2)}, u32[]{:S(2)}) %collective-permute-start.10) | collective-permute-done | bytes 1044512 | tf_op jit(solution)/shard_map/ppermute | solution.py:40
  272.5 33.3 %collective-permute-done.4 = bf16[680,768]{1,0:T(8,128)(2,1)} collective-permute-done((bf16[680,768]{1,0:T(8,128)(2,1)S(1)}, bf16[680,768]{1,0:T(8,128)(2,1)}, u32[]{:S(2)}, u32[]{:S(2)}) %collective-permute-start.4) | collective-permute-done | bytes 1044512 | tf_op jit(solution)/shard_map/ppermute | solution.py:38
  310.7 18.2 %collective-permute-done.11 = bf16[680,768]{1,0:T(8,128)(2,1)} collective-permute-done((bf16[680,768]{1,0:T(8,128)(2,1)}, bf16[680,768]{1,0:T(8,128)(2,1)}, u32[]{:S(2)}, u32[]{:S(2)}) %collective-permute-start.11) | collective-permute-done | bytes 1044512 | tf_op jit(solution)/shard_map/ppermute | solution.py:40
  328.8 34.8 %collective-permute-done.5 = bf16[680,768]{1,0:T(8,128)(2,1)} collective-permute-done((bf16[680,768]{1,0:T(8,128)(2,1)}, bf16[680,768]{1,0:T(8,128)(2,1)}, u32[]{:S(2)}, u32[]{:S(2)}) %collective-permute-start.5) | collective-permute-done | bytes 1044512 | tf_op jit(solution)/shard_map/ppermute | solution.py:38
  386.9 8.6 collective-permute-start.7
  395.5 86.9 %psum.28 = f32[]{:T(128)} all-reduce(f32[]{:T(128)} %convert_reduce_fusion.5), channel_id=1, replica_groups=mesh['dp'=16,'seq'=2] {'dp','seq'}, use_global_device_ids=true, to_apply=%region_23.24 | all-reduce | flops 1 | bytes 8 | tf_op jit(solution)/shard_map/psum | solution.py:342
  522.7 13.0 gather_fusion.1
  535.7 27.9 %reshape_reshape.3 = bf16[2720,4,768]{2,1,0:T(4,128)(2,1)} reshape(bf16[16,680,768]{2,1,0:T(8,128)(2,1)} %gather_fusion.1) | data formatting | bytes 33423360 | tf_op jit(solution)/shard_map/reshape;reshape | solution.py:93
  563.6 26.2 %gather_fusion.2 = bf16[2720,4,768]{2,1,0:T(4,128)(2,1)} fusion(bf16[2720,4,768]{2,1,0:T(4,128)(2,1)} %reshape_reshape.3, s32[3072]{0:T(1024)S(1)} %pad_clamp_fusion.1), kind=kCustom, calls=%fused_computation.2 | custom fusion | bytes 33434240 | tf_op jit(solution)/shard_map/gather | solution.py:93
  589.7 26.7 %reshape.863 = bf16[10880,768]{1,0:T(8,128)(2,1)} reshape(bf16[2720,4,768]{2,1,0:T(4,128)(2,1)} %gather_fusion.2) | data formatting | bytes 33423360 | tf_op jit(solution)/shard_map/reshape | solution.py:93
  642.9 10.6 fusion.165
  653.4 27.9 %reshape.858 = bf16[2720,4,768]{2,1,0:T(4,128)(2,1)} reshape(bf16[10880,768]{1,0:T(8,128)(2,1)} %all-gather.2.cloned.1.call-done) | data formatting | bytes 33423360 | tf_op jit(solution)/shard_map/reshape | solution.py:93
  681.4 26.2 %gather_fusion = bf16[2720,4,768]{2,1,0:T(4,128)(2,1)} fusion(bf16[2720,4,768]{2,1,0:T(4,128)(2,1)} %reshape.858, s32[3072]{0:T(1024)S(1)} %pad_clamp_fusion.1), kind=kCustom, calls=%fused_computation | custom fusion | bytes 33434240 | tf_op jit(solution)/shard_map/gather | solution.py:93
  712.5 26.8 %reshape.859 = bf16[10880,768]{1,0:T(8,128)(2,1)} reshape(bf16[2720,4,768]{2,1,0:T(4,128)(2,1)} %gather_fusion) | data formatting | bytes 33423360 | tf_op jit(solution)/shard_map/reshape | solution.py:93
  776.6 8.5 slice.211
  795.0 10.5 fusion.163
  805.5 9.0 slice.193
  889.9 11.8 reshape.886
  922.7 8.4 reshape.885
  933.3 78.6 %concatenate.9 = f32[10880,768]{1,0:T(8,128)} concatenate(f32[1,768]{1,0:T(1,128)S(1)} %reshape.871, f32[1,768]{1,0:T(1,128)S(1)} %reshape.872, f32[1,768]{1,0:T(1,128)S(1)} %reshape.873, f32[1,768]{1,0:T(1,128)S(1)} %reshape.874, f32[1,768]{1,0:T(1,128)S(1)} %reshape.875, f32[1,768]{1,0:T(1,128)S(1)} %copy-done.95, f32[1,768]{1,0:T(1,128)S(1)} %copy-done.96, ...), dimensions={0} | concatenate | bytes 66846720 | tf_op jit(solution)/shard_map/concatenate | solution.py:87
  1011.9 37.8 %reshape.887 = f32[2720,4,768]{2,1,0:T(4,128)} reshape(f32[10880,768]{1,0:T(8,128)} %concatenate.9) | data formatting | bytes 66846720 | tf_op jit(solution)/shard_map/reshape | solution.py:93
  1049.7 32.6 %gather_fusion.3 = f32[2720,4,768]{2,1,0:T(4,128)} fusion(f32[2720,4,768]{2,1,0:T(4,128)} %reshape.887, s32[3072]{0:T(1024)S(1)} %copy-done.73), kind=kCustom, calls=%fused_computation.3 | custom fusion | bytes 66857600 | tf_op jit(solution)/shard_map/gather | solution.py:93
  1082.3 38.5 %reshape.888 = f32[10880,768]{1,0:T(8,128)} reshape(f32[2720,4,768]{2,1,0:T(4,128)} %gather_fusion.3) | data formatting | bytes 66846720 | tf_op jit(solution)/shard_map/reshape | solution.py:93
  1120.9 494.0 %reduce-scatter.2.cloned.1.call-done = f32[680,768]{1,0:T(8,128)} async-done(((f32[10880,768]{1,0:T(8,128)}), f32[680,768]{1,0:T(8,128)}) %reduce-scatter.2.cloned.1.call-update) | async-done | bytes 2088976 | tf_op jit(solution)/shard_map/reduce_scatter | solution.py:405
  1616.4 21.5 %all-reduce.2.cloned.1.call-done = f32[680,768]{1,0:T(8,128)} async-done(((f32[680,768]{1,0:T(8,128)}), f32[680,768]{1,0:T(8,128)}) %all-reduce.2.cloned.1.call-update) | async-done | bytes 2088976 | tf_op jit(solution)/shard_map/psum | solution.py:406
  1640.6 40.4 %psum.29 = f32[]{:T(128)} all-reduce(f32[]{:T(128)S(6)} %mul.479), channel_id=1, replica_groups=mesh['dp'=16,'seq'=2] {'dp','seq'}, use_global_device_ids=true, to_apply=%region_24.25 | all-reduce | flops 1 | bytes 8 | tf_op jit(solution)/shard_map/psum | solution.py:383
  1681.1 41.3 %psum.31 = f32[]{:T(128)} all-reduce(f32[]{:T(128)} %multiply_reduce_fusion), channel_id=1, replica_groups=mesh['dp'=16,'seq'=2] {'dp'}, use_global_device_ids=true, to_apply=%region_49.50 | all-reduce | flops 1 | bytes 8 | tf_op jit(solution)/shard_map/psum | solution.py:407
  (459 shorter events, 273.4 us)
Async XLA Ops:
  7.2 627.0 %copy-start = (bf16[2,128,768]{2,1,0:T(8,128)(2,1)S(1)}, bf16[2,128,768]{2,1,0:T(8,128)(2,1)}, u32[]{:S(2)}) copy-start(bf16[2,128,768]{2,1,0:T(8,128)(2,1)} %param.9) | copy-start | bytes 1179652
  7.2 302.3 %copy-start.123 = (s32[2]{0:T(128)S(1)}, s32[2]{0:T(128)}, u32[]{:S(2)}) copy-start(s32[2]{0:T(128)} %param.11) | copy-start | bytes 28
  7.2 359.5 %copy-start.1 = (s32[2,196]{1,0:T(2,128)S(1)}, s32[2,196]{1,0:T(2,128)}, u32[]{:S(2)}) copy-start(s32[2,196]{1,0:T(2,128)} %param.10) | copy-start | bytes 4708
  7.2 362.6 %copy-start.74 = (s32[2720]{0:T(1024)S(1)}, s32[2720]{0:T(1024)}, u32[]{:S(2)}) copy-start(s32[2720]{0:T(1024)} %param.12) | copy-start | bytes 32644
  7.2 646.2 %all-gather.2.cloned.1.call-start = ((), (), s32[]{:S(2)}) async-start(), calls=%async_computation.1 | async-start | bytes 17756160 | tf_op jit(solution)/shard_map/all_gather | solution.py:328
  10.0 1604.8 %reduce-scatter.2.cloned.1.call-start = ((), (), s32[]{:S(2)}) async-start(), calls=%async_computation.2 | async-start | bytes 35512320 | tf_op jit(solution)/shard_map/reduce_scatter | solution.py:405
  10.1 41.7 %collective-permute-start = (bf16[680,768]{1,0:T(8,128)(2,1)S(1)}, bf16[680,768]{1,0:T(8,128)(2,1)S(1)}, u32[]{:S(2)}, u32[]{:S(2)}) collective-permute-start(bf16[680,768]{1,0:T(8,128)(2,1)S(1)} %copy-done.46), channel_id=1, source_target_pairs={{0,2},{2,4},{4,6},{6,8},{8,10},{10,12},{12,14},{14,16},{16,18},{18... | collective-permute-start | bytes 3133448 | tf_op jit(solution)/shard_map/ppermute | solution.py:38
  51.8 87.5 %collective-permute-start.1 = (bf16[680,768]{1,0:T(8,128)(2,1)S(1)}, bf16[680,768]{1,0:T(8,128)(2,1)S(1)}, u32[]{:S(2)}, u32[]{:S(2)}) collective-permute-start(bf16[680,768]{1,0:T(8,128)(2,1)S(1)} %collective-permute-done), channel_id=1, source_target_pairs={{0,2},{2,4},{4,6},{6,8},{8,10},{10,12},{12,14},{14,16},{16,18},{18... | collective-permute-start | bytes 3133448 | tf_op jit(solution)/shard_map/ppermute | solution.py:38
  51.8 90.5 %collective-permute-start.8 = (bf16[680,768]{1,0:T(8,128)(2,1)S(1)}, bf16[680,768]{1,0:T(8,128)(2,1)S(1)}, u32[]{:S(2)}, u32[]{:S(2)}) collective-permute-start(bf16[680,768]{1,0:T(8,128)(2,1)S(1)} %copy-done.46), channel_id=1, source_target_pairs={{2,0},{4,2},{6,4},{8,6},{10,8},{12,10},{14,12},{16,14},{18,16},{20... | collective-permute-start | bytes 3133448 | tf_op jit(solution)/shard_map/ppermute | solution.py:40
  139.3 55.3 %copy-start.47 = (bf16[680,768]{1,0:T(8,128)(2,1)}, bf16[680,768]{1,0:T(8,128)(2,1)S(1)}, u32[]{:S(2)}) copy-start(bf16[680,768]{1,0:T(8,128)(2,1)S(1)} %collective-permute-done.1) | copy-start | bytes 3133444
  139.3 30.8 %collective-permute-start.2 = (bf16[680,768]{1,0:T(8,128)(2,1)S(1)}, bf16[680,768]{1,0:T(8,128)(2,1)S(1)}, u32[]{:S(2)}, u32[]{:S(2)}) collective-permute-start(bf16[680,768]{1,0:T(8,128)(2,1)S(1)} %collective-permute-done.1), channel_id=1, source_target_pairs={{0,2},{2,4},{4,6},{6,8},{8,10},{10,12},{12,14},{14,16},{16,18},{18... | collective-permute-start | bytes 3133448 | tf_op jit(solution)/shard_map/ppermute | solution.py:38
  142.4 52.2 %collective-permute-start.9 = (bf16[680,768]{1,0:T(8,128)(2,1)S(1)}, bf16[680,768]{1,0:T(8,128)(2,1)S(1)}, u32[]{:S(2)}, u32[]{:S(2)}) collective-permute-start(bf16[680,768]{1,0:T(8,128)(2,1)S(1)} %collective-permute-done.8), channel_id=1, source_target_pairs={{2,0},{4,2},{6,4},{8,6},{10,8},{12,10},{14,12},{16,14},{18,16},{20... | collective-permute-start | bytes 3133448 | tf_op jit(solution)/shard_map/ppermute | solution.py:40
  170.1 102.4 %copy-start.51 = (bf16[680,768]{1,0:T(8,128)(2,1)}, bf16[680,768]{1,0:T(8,128)(2,1)S(1)}, u32[]{:S(2)}) copy-start(bf16[680,768]{1,0:T(8,128)(2,1)S(1)} %collective-permute-done.2) | copy-start | bytes 3133444
  170.1 69.4 %collective-permute-start.3 = (bf16[680,768]{1,0:T(8,128)(2,1)S(1)}, bf16[680,768]{1,0:T(8,128)(2,1)S(1)}, u32[]{:S(2)}, u32[]{:S(2)}) collective-permute-start(bf16[680,768]{1,0:T(8,128)(2,1)S(1)} %collective-permute-done.2), channel_id=1, source_target_pairs={{0,2},{2,4},{4,6},{6,8},{8,10},{10,12},{12,14},{14,16},{16,18},{18... | collective-permute-start | bytes 3133448 | tf_op jit(solution)/shard_map/ppermute | solution.py:38
  194.6 78.0 %collective-permute-start.10 = (bf16[680,768]{1,0:T(8,128)(2,1)S(1)}, bf16[680,768]{1,0:T(8,128)(2,1)}, u32[]{:S(2)}, u32[]{:S(2)}) collective-permute-start(bf16[680,768]{1,0:T(8,128)(2,1)S(1)} %collective-permute-done.9), channel_id=1, source_target_pairs={{2,0},{4,2},{6,4},{8,6},{10,8},{12,10},{14,12},{16,14},{18,16},{20... | collective-permute-start | bytes 3133448 | tf_op jit(solution)/shard_map/ppermute | solution.py:40
  239.4 33.1 %copy-start.53 = (bf16[680,768]{1,0:T(8,128)(2,1)}, bf16[680,768]{1,0:T(8,128)(2,1)S(1)}, u32[]{:S(2)}) copy-start(bf16[680,768]{1,0:T(8,128)(2,1)S(1)} %collective-permute-done.3) | copy-start | bytes 3133444
  239.4 66.4 %collective-permute-start.4 = (bf16[680,768]{1,0:T(8,128)(2,1)S(1)}, bf16[680,768]{1,0:T(8,128)(2,1)}, u32[]{:S(2)}, u32[]{:S(2)}) collective-permute-start(bf16[680,768]{1,0:T(8,128)(2,1)S(1)} %collective-permute-done.3), channel_id=1, source_target_pairs={{0,2},{2,4},{4,6},{6,8},{8,10},{10,12},{12,14},{14,16},{16,18},{18... | collective-permute-start | bytes 3133448 | tf_op jit(solution)/shard_map/ppermute | solution.py:38
  272.5 56.3 %collective-permute-start.11 = (bf16[680,768]{1,0:T(8,128)(2,1)}, bf16[680,768]{1,0:T(8,128)(2,1)}, u32[]{:S(2)}, u32[]{:S(2)}) collective-permute-start(bf16[680,768]{1,0:T(8,128)(2,1)} %collective-permute-done.10), channel_id=1, source_target_pairs={{2,0},{4,2},{6,4},{8,6},{10,8},{12,10},{14,12},{16,14},{18,16},{20... | collective-permute-start | bytes 3133448 | tf_op jit(solution)/shard_map/ppermute | solution.py:40
  305.8 57.8 %collective-permute-start.5 = (bf16[680,768]{1,0:T(8,128)(2,1)}, bf16[680,768]{1,0:T(8,128)(2,1)}, u32[]{:S(2)}, u32[]{:S(2)}) collective-permute-start(bf16[680,768]{1,0:T(8,128)(2,1)} %collective-permute-done.4), channel_id=1, source_target_pairs={{0,2},{2,4},{4,6},{6,8},{8,10},{10,12},{12,14},{14,16},{16,18},{18... | collective-permute-start | bytes 3133448 | tf_op jit(solution)/shard_map/ppermute | solution.py:38
  309.5 69.4 %copy-start.106 = (pred[128]{0:T(512)(128)(4,1)}, pred[128]{0:T(512)(128)(4,1)S(1)}, u32[]{:S(2)}) copy-start(pred[128]{0:T(512)(128)(4,1)S(1)} %get-tuple-element.126) | copy-start | bytes 388
  310.6 55.5 %copy-start.107 = (s32[2]{0:T(128)}, s32[2]{0:T(128)S(1)}, u32[]{:S(2)}) copy-start(s32[2]{0:T(128)S(1)} %get-tuple-element.93) | copy-start | bytes 28
  328.8 52.0 %collective-permute-start.12 = (bf16[680,768]{1,0:T(8,128)(2,1)}, bf16[680,768]{1,0:T(8,128)(2,1)}, u32[]{:S(2)}, u32[]{:S(2)}) collective-permute-start(bf16[680,768]{1,0:T(8,128)(2,1)} %collective-permute-done.11), channel_id=1, source_target_pairs={{2,0},{4,2},{6,4},{8,6},{10,8},{12,10},{14,12},{16,14},{18,16},{20... | collective-permute-start | bytes 3133448 | tf_op jit(solution)/shard_map/ppermute | solution.py:40
  363.7 23.2 %collective-permute-start.6 = (bf16[680,768]{1,0:T(8,128)(2,1)}, bf16[680,768]{1,0:T(8,128)(2,1)}, u32[]{:S(2)}, u32[]{:S(2)}) collective-permute-start(bf16[680,768]{1,0:T(8,128)(2,1)} %collective-permute-done.5), channel_id=1, source_target_pairs={{0,2},{2,4},{4,6},{6,8},{8,10},{10,12},{12,14},{14,16},{16,18},{18... | collective-permute-start | bytes 3133448 | tf_op jit(solution)/shard_map/ppermute | solution.py:38
  380.9 109.9 %collective-permute-start.13 = (bf16[680,768]{1,0:T(8,128)(2,1)}, bf16[680,768]{1,0:T(8,128)(2,1)}, u32[]{:S(2)}, u32[]{:S(2)}) collective-permute-start(bf16[680,768]{1,0:T(8,128)(2,1)} %collective-permute-done.12), channel_id=1, source_target_pairs={{2,0},{4,2},{6,4},{8,6},{10,8},{12,10},{14,12},{16,14},{18,16},{20... | collective-permute-start | bytes 3133448 | tf_op jit(solution)/shard_map/ppermute | solution.py:40
  386.9 108.9 %collective-permute-start.7 = (bf16[680,768]{1,0:T(8,128)(2,1)}, bf16[680,768]{1,0:T(8,128)(2,1)}, u32[]{:S(2)}, u32[]{:S(2)}) collective-permute-start(bf16[680,768]{1,0:T(8,128)(2,1)} %collective-permute-done.6), channel_id=1, source_target_pairs={{0,2},{2,4},{4,6},{6,8},{8,10},{10,12},{12,14},{14,16},{16,18},{18... | collective-permute-start | bytes 3133448 | tf_op jit(solution)/shard_map/ppermute | solution.py:38
  490.8 30.8 %collective-permute-start.14 = (bf16[680,768]{1,0:T(8,128)(2,1)}, bf16[680,768]{1,0:T(8,128)(2,1)S(1)}, u32[]{:S(2)}, u32[]{:S(2)}) collective-permute-start(bf16[680,768]{1,0:T(8,128)(2,1)} %collective-permute-done.13), channel_id=1, source_target_pairs={{2,0},{4,2},{6,4},{8,6},{10,8},{12,10},{14,12},{16,14},{18,16},{20... | collective-permute-start | bytes 3133448 | tf_op jit(solution)/shard_map/ppermute | solution.py:40
  772.8 50.8 %collective-permute-start.15 = (bf16[4,2,128,12,64]{2,4,3,1,0:T(8,128)(2,1)}, bf16[4,2,128,12,64]{2,4,3,1,0:T(8,128)(2,1)}, u32[]{:S(2)}, u32[]{:S(2)}) collective-permute-start(bf16[4,2,128,12,64]{2,4,3,1,0:T(8,128)(2,1)} %pad_maximum_fusion), channel_id=1, source_target_pairs={{0,1},{1,0},{2,3},{3,2},{4,5},{5,4},{6,7},{7,6},{8,9},{9,8},{10,11... | collective-permute-start | bytes 4718600 | tf_op jit(solution)/shard_map/ppermute | solution.py:48
  844.2 17.1 copy-start.8
  884.3 26.7 %collective-permute-start.16 = (bf16[2,2,128,12,64]{2,4,3,1,0:T(8,128)(2,1)}, bf16[2,2,128,12,64]{2,4,3,1,0:T(8,128)(2,1)}, u32[]{:S(2)}, u32[]{:S(2)}) collective-permute-start(bf16[2,2,128,12,64]{2,4,3,1,0:T(8,128)(2,1)} %pad_maximum_fusion.2), channel_id=1, source_target_pairs={{0,1},{1,0},{2,3},{3,2},{4,5},{5,4},{6,7},{7,6},{8,9},{9,8},{10,11... | collective-permute-start | bytes 2359304 | tf_op jit(solution)/shard_map/ppermute | solution.py:48
  1011.9 37.8 %copy-start.73 = (s32[3072]{0:T(1024)S(1)}, s32[3072]{0:T(1024)}, u32[]{:S(2)}) copy-start(s32[3072]{0:T(1024)} %pad_clamp_fusion) | copy-start | bytes 36868
  1120.8 517.0 %all-reduce.2.cloned.1.call-start = ((), (), s32[]{:S(2)}) async-start(), calls=%async_computation.3 | async-start | bytes 4177920 | tf_op jit(solution)/shard_map/psum | solution.py:406
  1614.9 108.2 %copy-start.14 = (f32[680,768]{1,0:T(8,128)S(1)}, f32[680,768]{1,0:T(8,128)}, u32[]{:S(2)}) copy-start(f32[680,768]{1,0:T(8,128)} %param.13) | copy-start | bytes 6266884
  (119 other events, 418.3 us)
Sparse Core Ops, SparseCore 0:
  10.8 342.0 all-gather.1
  1121.0 493.8 reduce-scatter.1
  1617.2 20.6 all-reduce.1
